TPU v7x, 8 devices: a whole 2x2x1 slice. The times are simulated.
8 devices in a mesh: tasks: 1 (over z), group: 8 (over y, x, core).
Axes of the slice: x: 2, y: 2, z: 1, core: 2. Of those that a mesh axis runs over, the one named last changes fastest.
Arguments:
- points: bfloat16 [16384, 512], P(('tasks', 'group'))
- vectors: bfloat16 [16384, 128], P(('tasks', 'group'))
- lengthscale: float32 [1], replicated
- outscale: float32 [1], replicated
Outputs:
- output: float32 [16384, 128], P(('tasks', 'group'))
All inputs are finite; a program needn't handle non-finite values.
Results may differ from a plain program's by a relative error of at most 0.001.
Values are sent between devices in bfloat16 or wider.
A program may use at most 1 GiB of HBM per device.

v0:
```python
import jax
import jax.numpy as jnp
from jax import lax
from jax.sharding import PartitionSpec as P


def row_norms(x_rows):
    return jnp.sum(jnp.square(x_rows.astype(jnp.float32)), axis=1)


def kernel_block(x_rows, norm_rows, x_cols, norm_cols, two_ell_sq, out_scale):
    gram_mat = jnp.einsum('nd,md->nm', x_rows, x_cols, preferred_element_type=jnp.float32)
    sq_dist = jnp.maximum(norm_rows[:, None] + norm_cols[None, :] - 2.0 * gram_mat, 0.0)
    return (out_scale * jnp.exp(-sq_dist / two_ell_sq)).astype(jnp.bfloat16)


def solution(mesh):
    n_group = mesh.shape['group']
    half_way = n_group // 2
    shift_left = [(source_idx, (source_idx - 1) % n_group) for source_idx in range(n_group)]
    send_back = [(source_idx, (source_idx + half_way - 1) % n_group) for source_idx in range(n_group)]
    row_spec = P(('tasks', 'group'), None)

    def local_fn(x_loc, v_loc, lengthscale, outscale):
        two_ell_sq = 2.0 * jnp.square(lengthscale[0])
        out_scale = outscale[0]
        norm_loc = row_norms(x_loc)

        def pair_step(x_vis, v_vis, y_acc, partner_acc):
            kern_pair = kernel_block(x_loc, norm_loc, x_vis, row_norms(x_vis), two_ell_sq, out_scale)
            y_acc = y_acc + jnp.dot(kern_pair, v_vis, preferred_element_type=jnp.float32)
            partner_acc = partner_acc + jnp.einsum('nm,nr->mr', kern_pair, v_loc, preferred_element_type=jnp.float32)
            return y_acc, partner_acc

        def loop_body(step_idx, carry):
            x_vis, v_vis, y_acc, partner_acc = carry
            x_vis = lax.ppermute(x_vis, 'group', shift_left)
            v_vis = lax.ppermute(v_vis, 'group', shift_left)
            partner_acc = lax.ppermute(partner_acc, 'group', shift_left)
            y_acc, partner_acc = pair_step(x_vis, v_vis, y_acc, partner_acc)
            return x_vis, v_vis, y_acc, partner_acc

        kern_diag = kernel_block(x_loc, norm_loc, x_loc, norm_loc, two_ell_sq, out_scale)
        y_acc = jnp.dot(kern_diag, v_loc, preferred_element_type=jnp.float32)
        x_vis = lax.ppermute(x_loc, 'group', shift_left)
        v_vis = lax.ppermute(v_loc, 'group', shift_left)
        y_acc, partner_acc = pair_step(x_vis, v_vis, y_acc, jnp.zeros(y_acc.shape, jnp.float32))
        x_vis, v_vis, y_acc, partner_acc = lax.fori_loop(2, half_way, loop_body, (x_vis, v_vis, y_acc, partner_acc))
        y_acc = y_acc + lax.ppermute(partner_acc, 'group', send_back)
        x_vis = lax.ppermute(x_vis, 'group', shift_left)
        v_vis = lax.ppermute(v_vis, 'group', shift_left)
        kern_far = kernel_block(x_loc, norm_loc, x_vis, row_norms(x_vis), two_ell_sq, out_scale)
        return y_acc + jnp.dot(kern_far, v_vis, preferred_element_type=jnp.float32)

    return jax.shard_map(local_fn, mesh=mesh, in_specs=(row_spec, row_spec, P(None), P(None)), out_specs=row_spec, check_vma=False)
```

profile of v0, /device:TPU:0, one launch (start us, length us, event | category | flops | bytes accessed | tf_op | source)
XLA Modules:
  0.0 261.6 jit_solution(4724699184030770555)
XLA Ops:
  0.0 3.7 %collective-permute-start.3 = (bf16[2048,512]{1,0:T(8,128)(2,1)}, bf16[2048,512]{1,0:T(8,128)(2,1)S(1)}, u32[]{:S(2)}, u32[]{:S(2)}) collective-permute-start(bf16[2048,512]{1,0:T(8,128)(2,1)} %param.6), channel_id=1, source_target_pairs={{0,7},{1,0},{2,1},{3,2},{4,3},{5,4},{6,5},{7,6}} | collective-permute-start | bytes 6291464 | tf_op jit(solution)/shard_map/ppermute | solution.py:45
  3.7 0.7 collective-permute-start.4
  4.4 2.1 multiply_reduce_fusion.3
  6.5 12.5 %multiply_subtract_fusion = f32[2048,2048]{0,1:T(8,128)} fusion(bf16[2048,512]{1,0:T(8,128)(2,1)} %param.6, f32[2048]{0:T(1024)S(1)} %multiply_reduce_fusion.3), kind=kOutput, calls=%fused_computation.12 | convolution fusion | flops 4307550208 | bytes 18882560 | tf_op jit(solution)/shard_map/nd,md->nm/dot_general | solution.py:12
  19.0 17.7 %copy.5 = f32[2048,2048]{1,0:T(8,128)} copy(f32[2048,2048]{0,1:T(8,128)} %multiply_subtract_fusion) | data formatting | bytes 33554432 | tf_op jit(solution)/shard_map/sub | solution.py:13
  38.0 8.7 %fusion.9 = f32[2048,128]{1,0:T(8,128)} fusion(bf16[2048,128]{1,0:T(8,128)(2,1)S(1)} %copy-done, f32[2048,2048]{1,0:T(8,128)} %copy.5, f32[]{:T(128)} %bitcast.1, f32[]{:T(128)} %bitcast.50), kind=kOutput, calls=%fused_computation.19 | convolution fusion | flops 1094713344 | bytes 18350088 | tf_op jit(solution)/shard_map/dot_general | solution.py:44
  46.8 0.0 collective-permute-done.3
  46.8 0.5 multiply_reduce_fusion.2
  47.2 0.8 copy-done.4
  48.1 6.9 %broadcast_add_fusion.1 = f32[2048,2048]{0,1:T(8,128)} fusion(f32[2048]{0:T(1024)S(1)} %multiply_reduce_fusion.2, f32[2048]{0:T(1024)S(1)} %multiply_reduce_fusion.3), kind=kLoop, calls=%fused_computation.15 | loop fusion | flops 4194304 | bytes 16793600 | tf_op jit(solution)/shard_map/add | solution.py:13
  55.0 17.8 %copy.7 = f32[2048,2048]{1,0:T(8,128)} copy(f32[2048,2048]{0,1:T(8,128)} %broadcast_add_fusion.1) | data formatting | bytes 33554432 | tf_op jit(solution)/shard_map/add | solution.py:13
  72.8 10.7 %multiply_convert_fusion.1 = bf16[2048,2048]{1,0:T(8,128)(2,1)S(1)} fusion(f32[2048,2048]{1,0:T(8,128)} %copy.7, bf16[2048,512]{1,0:T(8,128)(2,1)S(1)} %copy-done.2, bf16[2048,512]{1,0:T(8,128)(2,1)} %copy-done.4, f32[]{:T(128)} %bitcast.1, f32[]{:T(128)} %bitcast.52), kind=kOutput, calls=%fused_computation.10 | convolution fusion | flops 4324327424 | bytes 29360136 | tf_op jit(solution)/shard_map/nd,md->nm/dot_general | solution.py:12
  83.5 3.5 %fusion.13 = f32[2048,128]{1,0:T(8,128)} fusion(bf16[2048,2048]{1,0:T(8,128)(2,1)S(1)} %multiply_convert_fusion.1, bf16[2048,128]{1,0:T(8,128)(2,1)S(1)} %copy-done), kind=kOutput, calls=%fused_computation.28 | convolution fusion | flops 1073741824 | bytes 9961472 | tf_op jit(solution)/shard_map/nm,nr->mr/dot_general | solution.py:32
  87.0 3.4 %convolution_add_fusion.2 = f32[2048,128]{1,0:T(8,128)S(1)} fusion(f32[2048,128]{1,0:T(8,128)S(1)} %copy-done.6, bf16[2048,2048]{1,0:T(8,128)(2,1)S(1)} %multiply_convert_fusion.1, bf16[2048,128]{1,0:T(8,128)(2,1)} %collective-permute-done.4), kind=kOutput, calls=%fused_computation.23 | convolution fusion | flops 1074003968 | bytes 11010048 | tf_op jit(solution)/shard_map/dot_general | solution.py:31
  90.4 102.5 %while.16 = (s32[]{:T(128)}, bf16[2048,512]{1,0:T(8,128)(2,1)}, bf16[2048,128]{1,0:T(8,128)(2,1)}, f32[2048,128]{1,0:T(8,128)S(1)}, f32[2048,128]{1,0:T(8,128)},...) while((s32[]{:T(128)}, bf16[2048,512]{1,0:T(8,128)(2,1)}, ...), condition=%wide.region_4.0_spmd, body=%wide.region_2.0_spmd.sunk | while | flops 6479673344 | bytes 58745096 | solution.py:48
  90.4 0.0 collective-permute-start
  90.5 0.6 collective-permute-start.1
  91.1 0.9 collective-permute-start.2
  92.0 27.6 %collective-permute-done.1 = bf16[2048,128]{1,0:T(8,128)(2,1)} collective-permute-done((bf16[2048,128]{1,0:T(8,128)(2,1)}, bf16[2048,128]{1,0:T(8,128)(2,1)}, u32[]{:S(2)}, u32[]{:S(2)}) %collective-permute-start.1) | collective-permute-done | bytes 524320 | tf_op jit(solution)/shard_map/while/body/eval_jaxpr/ppermute | solution.py:38
  119.6 1.9 copy.21
  121.5 0.0 collective-permute-done
  121.5 0.5 multiply_reduce_fusion.5
  122.0 8.8 %multiply_convert_fusion.5 = bf16[2048,2048]{1,0:T(8,128)(2,1)S(1)} fusion(bf16[2048,512]{1,0:T(8,128)(2,1)} %get-tuple-element.174, bf16[2048,512]{1,0:T(8,128)(2,1)S(1)} %collective-permute-done, f32[]{:T(128)} %get-tuple-element.175, f32[2048]{0:T(1024)S(1)} %multiply_reduce_fusion.5, f32[2048]{0:T(1024)S(1)} %get-tuple-element.173, ...), kind=kOutput, calls=%fused_computation.clone.1 | convolution fusion | flops 4328521728 | bytes 12599304 | tf_op jit(solution)/shard_map/while/body/eval_jaxpr/nd,md->nm/dot_general | solution.py:12
  130.8 0.0 copy-start.1
  130.8 1.3 copy.20
  132.1 3.4 %convolution_add_fusion.5 = f32[2048,128]{1,0:T(8,128)S(1)} fusion(f32[2048,128]{1,0:T(8,128)S(1)} %get-tuple-element.159, bf16[2048,2048]{1,0:T(8,128)(2,1)S(1)} %multiply_convert_fusion.5, bf16[2048,128]{1,0:T(8,128)(2,1)} %collective-permute-done.1), kind=kOutput, calls=%fused_computation.3.clone.1 | convolution fusion | flops 1074003968 | bytes 11010048 | tf_op jit(solution)/shard_map/while/body/eval_jaxpr/dot_general | solution.py:31
  135.5 0.0 collective-permute-done.2
  135.6 4.7 %convolution_add_fusion.6 = f32[2048,128]{1,0:T(8,128)} fusion(f32[2048,128]{1,0:T(8,128)} %collective-permute-done.2, bf16[2048,2048]{1,0:T(8,128)(2,1)S(1)} %multiply_convert_fusion.5, bf16[2048,128]{1,0:T(8,128)(2,1)S(1)} %copy-done.1), kind=kOutput, calls=%fused_computation.2.clone.1 | convolution fusion | flops 1074003968 | bytes 11010048 | tf_op jit(solution)/shard_map/while/body/eval_jaxpr/nm,nr->mr/dot_general | solution.py:32
  140.3 2.8 %collective-permute-start = (bf16[2048,512]{1,0:T(8,128)(2,1)}, bf16[2048,512]{1,0:T(8,128)(2,1)S(1)}, u32[]{:S(2)}, u32[]{:S(2)}) collective-permute-start(bf16[2048,512]{1,0:T(8,128)(2,1)} %get-tuple-element.157), channel_id=1, source_target_pairs={{0,7},{1,0},{2,1},{3,2},{4,3},{5,4},{6,5},{7,6}} | collective-permute-start | bytes 6291464 | tf_op jit(solution)/shard_map/while/body/eval_jaxpr/ppermute | solution.py:37
  143.1 0.0 collective-permute-start.1
  143.2 0.6 collective-permute-start.2
  143.7 28.5 %collective-permute-done.1 = bf16[2048,128]{1,0:T(8,128)(2,1)} collective-permute-done((bf16[2048,128]{1,0:T(8,128)(2,1)}, bf16[2048,128]{1,0:T(8,128)(2,1)}, u32[]{:S(2)}, u32[]{:S(2)}) %collective-permute-start.1) | collective-permute-done | bytes 524320 | tf_op jit(solution)/shard_map/while/body/eval_jaxpr/ppermute | solution.py:38
  172.3 1.9 copy.21
  174.1 0.0 collective-permute-done
  174.1 0.5 multiply_reduce_fusion.5
  174.6 8.8 %multiply_convert_fusion.5 = bf16[2048,2048]{1,0:T(8,128)(2,1)S(1)} fusion(bf16[2048,512]{1,0:T(8,128)(2,1)} %get-tuple-element.174, bf16[2048,512]{1,0:T(8,128)(2,1)S(1)} %collective-permute-done, f32[]{:T(128)} %get-tuple-element.175, f32[2048]{0:T(1024)S(1)} %multiply_reduce_fusion.5, f32[2048]{0:T(1024)S(1)} %get-tuple-element.173, ...), kind=kOutput, calls=%fused_computation.clone.1 | convolution fusion | flops 4328521728 | bytes 12599304 | tf_op jit(solution)/shard_map/while/body/eval_jaxpr/nd,md->nm/dot_general | solution.py:12
  183.4 0.0 copy-start.1
  183.4 1.3 copy.20
  184.8 3.4 %convolution_add_fusion.5 = f32[2048,128]{1,0:T(8,128)S(1)} fusion(f32[2048,128]{1,0:T(8,128)S(1)} %get-tuple-element.159, bf16[2048,2048]{1,0:T(8,128)(2,1)S(1)} %multiply_convert_fusion.5, bf16[2048,128]{1,0:T(8,128)(2,1)} %collective-permute-done.1), kind=kOutput, calls=%fused_computation.3.clone.1 | convolution fusion | flops 1074003968 | bytes 11010048 | tf_op jit(solution)/shard_map/while/body/eval_jaxpr/dot_general | solution.py:31
  188.2 4.7 %convolution_add_fusion.6 = f32[2048,128]{1,0:T(8,128)} fusion(f32[2048,128]{1,0:T(8,128)} %collective-permute-done.2, bf16[2048,2048]{1,0:T(8,128)(2,1)S(1)} %multiply_convert_fusion.5, bf16[2048,128]{1,0:T(8,128)(2,1)S(1)} %copy-done.1), kind=kOutput, calls=%fused_computation.2.clone.1 | convolution fusion | flops 1074003968 | bytes 11010048 | tf_op jit(solution)/shard_map/while/body/eval_jaxpr/nm,nr->mr/dot_general | solution.py:32
  192.9 2.8 %collective-permute-start.6 = (bf16[2048,512]{1,0:T(8,128)(2,1)}, bf16[2048,512]{1,0:T(8,128)(2,1)S(1)}, u32[]{:S(2)}, u32[]{:S(2)}) collective-permute-start(bf16[2048,512]{1,0:T(8,128)(2,1)} %get-tuple-element.62), channel_id=1, source_target_pairs={{0,7},{1,0},{2,1},{3,2},{4,3},{5,4},{6,5},{7,6}} | collective-permute-start | bytes 6291464 | tf_op jit(solution)/shard_map/ppermute | solution.py:50
  195.8 0.8 collective-permute-start.7
  196.6 22.8 %collective-permute-done.6 = bf16[2048,512]{1,0:T(8,128)(2,1)S(1)} collective-permute-done((bf16[2048,512]{1,0:T(8,128)(2,1)}, bf16[2048,512]{1,0:T(8,128)(2,1)S(1)}, u32[]{:S(2)}, u32[]{:S(2)}) %collective-permute-start.6) | collective-permute-done | bytes 2097184 | tf_op jit(solution)/shard_map/ppermute | solution.py:50
  219.4 1.3 copy-done.5
  220.7 0.5 multiply_reduce_fusion.1
  221.2 6.9 %broadcast_add_fusion = f32[2048,2048]{0,1:T(8,128)} fusion(f32[2048]{0:T(1024)S(1)} %multiply_reduce_fusion.1, f32[2048]{0:T(1024)S(1)} %get-tuple-element.186), kind=kLoop, calls=%fused_computation.14 | loop fusion | flops 4194304 | bytes 16793600 | tf_op jit(solution)/shard_map/add | solution.py:13
  228.1 17.8 %copy.8 = f32[2048,2048]{1,0:T(8,128)} copy(f32[2048,2048]{0,1:T(8,128)} %broadcast_add_fusion) | data formatting | bytes 33554432 | tf_op jit(solution)/shard_map/add | solution.py:13
  245.8 15.7 %add_add_fusion = f32[2048,128]{1,0:T(8,128)} fusion(f32[2048,128]{1,0:T(8,128)S(1)} %get-tuple-element.60, f32[2048,128]{1,0:T(8,128)} %collective-permute-done.5, bf16[2048,128]{1,0:T(8,128)(2,1)} %collective-permute-done.7, f32[2048,2048]{1,0:T(8,128)} %copy.8, bf16[2048,512]{1,0:T(8,128)(2,1)} %copy-done.5, bf16[2048,512]{1,0:T(8,128)(2,1)S(1)} %copy-done.3, ...), kind=kOutput, calls=%fused_computation.24 | convolution fusion | flops 5398593536 | bytes 24641544 | tf_op jit(solution)/shard_map/dot_general | solution.py:53
  (17 shorter events, 0.0 us)
Async XLA Ops:
  0.0 46.8 %collective-permute-start.3 = (bf16[2048,512]{1,0:T(8,128)(2,1)}, bf16[2048,512]{1,0:T(8,128)(2,1)S(1)}, u32[]{:S(2)}, u32[]{:S(2)}) collective-permute-start(bf16[2048,512]{1,0:T(8,128)(2,1)} %param.6), channel_id=1, source_target_pairs={{0,7},{1,0},{2,1},{3,2},{4,3},{5,4},{6,5},{7,6}} | collective-permute-start | bytes 6291464 | tf_op jit(solution)/shard_map/ppermute | solution.py:45
  3.7 83.2 %collective-permute-start.4 = (bf16[2048,128]{1,0:T(8,128)(2,1)}, bf16[2048,128]{1,0:T(8,128)(2,1)}, u32[]{:S(2)}, u32[]{:S(2)}) collective-permute-start(bf16[2048,128]{1,0:T(8,128)(2,1)} %param.7), channel_id=1, source_target_pairs={{0,7},{1,0},{2,1},{3,2},{4,3},{5,4},{6,5},{7,6}} | collective-permute-start | bytes 1572872 | tf_op jit(solution)/shard_map/ppermute | solution.py:46
  19.0 19.0 %copy-start = (bf16[2048,128]{1,0:T(8,128)(2,1)S(1)}, bf16[2048,128]{1,0:T(8,128)(2,1)}, u32[]{:S(2)}) copy-start(bf16[2048,128]{1,0:T(8,128)(2,1)} %param.7) | copy-start | bytes 1572868
  46.8 1.3 copy-start.4
  55.0 17.8 %copy-start.2 = (bf16[2048,512]{1,0:T(8,128)(2,1)S(1)}, bf16[2048,512]{1,0:T(8,128)(2,1)}, u32[]{:S(2)}) copy-start(bf16[2048,512]{1,0:T(8,128)(2,1)} %param.6) | copy-start | bytes 6291460
  72.8 14.2 %copy-start.6 = (f32[2048,128]{1,0:T(8,128)S(1)}, f32[2048,128]{1,0:T(8,128)}, u32[]{:S(2)}) copy-start(f32[2048,128]{1,0:T(8,128)} %fusion.9) | copy-start | bytes 3145732
  90.4 31.1 %collective-permute-start = (bf16[2048,512]{1,0:T(8,128)(2,1)}, bf16[2048,512]{1,0:T(8,128)(2,1)S(1)}, u32[]{:S(2)}, u32[]{:S(2)}) collective-permute-start(bf16[2048,512]{1,0:T(8,128)(2,1)} %get-tuple-element.157), channel_id=1, source_target_pairs={{0,7},{1,0},{2,1},{3,2},{4,3},{5,4},{6,5},{7,6}} | collective-permute-start | bytes 6291464 | tf_op jit(solution)/shard_map/while/body/eval_jaxpr/ppermute | solution.py:37
  90.5 29.1 %collective-permute-start.1 = (bf16[2048,128]{1,0:T(8,128)(2,1)}, bf16[2048,128]{1,0:T(8,128)(2,1)}, u32[]{:S(2)}, u32[]{:S(2)}) collective-permute-start(bf16[2048,128]{1,0:T(8,128)(2,1)} %get-tuple-element.158), channel_id=1, source_target_pairs={{0,7},{1,0},{2,1},{3,2},{4,3},{5,4},{6,5},{7,6}} | collective-permute-start | bytes 1572872 | tf_op jit(solution)/shard_map/while/body/eval_jaxpr/ppermute | solution.py:38
  91.1 44.4 %collective-permute-start.2 = (f32[2048,128]{1,0:T(8,128)}, f32[2048,128]{1,0:T(8,128)}, u32[]{:S(2)}, u32[]{:S(2)}) collective-permute-start(f32[2048,128]{1,0:T(8,128)} %get-tuple-element.160), channel_id=1, source_target_pairs={{0,7},{1,0},{2,1},{3,2},{4,3},{5,4},{6,5},{7,6}} | collective-permute-start | bytes 3145736 | tf_op jit(solution)/shard_map/while/body/eval_jaxpr/ppermute | solution.py:39
  130.8 4.8 %copy-start.1 = (bf16[2048,128]{1,0:T(8,128)(2,1)S(1)}, bf16[2048,128]{1,0:T(8,128)(2,1)}, u32[]{:S(2)}) copy-start(bf16[2048,128]{1,0:T(8,128)(2,1)} %get-tuple-element.176) | copy-start | bytes 1572868 | tf_op jit(solution)/shard_map/while
  140.3 33.9 %collective-permute-start = (bf16[2048,512]{1,0:T(8,128)(2,1)}, bf16[2048,512]{1,0:T(8,128)(2,1)S(1)}, u32[]{:S(2)}, u32[]{:S(2)}) collective-permute-start(bf16[2048,512]{1,0:T(8,128)(2,1)} %get-tuple-element.157), channel_id=1, source_target_pairs={{0,7},{1,0},{2,1},{3,2},{4,3},{5,4},{6,5},{7,6}} | collective-permute-start | bytes 6291464 | tf_op jit(solution)/shard_map/while/body/eval_jaxpr/ppermute | solution.py:37
  143.1 29.1 %collective-permute-start.1 = (bf16[2048,128]{1,0:T(8,128)(2,1)}, bf16[2048,128]{1,0:T(8,128)(2,1)}, u32[]{:S(2)}, u32[]{:S(2)}) collective-permute-start(bf16[2048,128]{1,0:T(8,128)(2,1)} %get-tuple-element.158), channel_id=1, source_target_pairs={{0,7},{1,0},{2,1},{3,2},{4,3},{5,4},{6,5},{7,6}} | collective-permute-start | bytes 1572872 | tf_op jit(solution)/shard_map/while/body/eval_jaxpr/ppermute | solution.py:38
  143.2 45.0 %collective-permute-start.2 = (f32[2048,128]{1,0:T(8,128)}, f32[2048,128]{1,0:T(8,128)}, u32[]{:S(2)}, u32[]{:S(2)}) collective-permute-start(f32[2048,128]{1,0:T(8,128)} %get-tuple-element.160), channel_id=1, source_target_pairs={{0,7},{1,0},{2,1},{3,2},{4,3},{5,4},{6,5},{7,6}} | collective-permute-start | bytes 3145736 | tf_op jit(solution)/shard_map/while/body/eval_jaxpr/ppermute | solution.py:39
  183.4 4.8 %copy-start.1 = (bf16[2048,128]{1,0:T(8,128)(2,1)S(1)}, bf16[2048,128]{1,0:T(8,128)(2,1)}, u32[]{:S(2)}) copy-start(bf16[2048,128]{1,0:T(8,128)(2,1)} %get-tuple-element.176) | copy-start | bytes 1572868 | tf_op jit(solution)/shard_map/while
  192.9 26.4 %collective-permute-start.6 = (bf16[2048,512]{1,0:T(8,128)(2,1)}, bf16[2048,512]{1,0:T(8,128)(2,1)S(1)}, u32[]{:S(2)}, u32[]{:S(2)}) collective-permute-start(bf16[2048,512]{1,0:T(8,128)(2,1)} %get-tuple-element.62), channel_id=1, source_target_pairs={{0,7},{1,0},{2,1},{3,2},{4,3},{5,4},{6,5},{7,6}} | collective-permute-start | bytes 6291464 | tf_op jit(solution)/shard_map/ppermute | solution.py:50
  195.8 50.1 %collective-permute-start.5 = (f32[2048,128]{1,0:T(8,128)}, f32[2048,128]{1,0:T(8,128)}, u32[]{:S(2)}, u32[]{:S(2)}) collective-permute-start(f32[2048,128]{1,0:T(8,128)} %get-tuple-element.61), channel_id=1, source_target_pairs={{0,3},{1,4},{2,5},{3,6},{4,7},{5,0},{6,1},{7,2}} | collective-permute-start | bytes 3145736 | tf_op jit(solution)/shard_map/ppermute | solution.py:49
  195.8 50.1 %collective-permute-start.7 = (bf16[2048,128]{1,0:T(8,128)(2,1)}, bf16[2048,128]{1,0:T(8,128)(2,1)}, u32[]{:S(2)}, u32[]{:S(2)}) collective-permute-start(bf16[2048,128]{1,0:T(8,128)(2,1)} %get-tuple-element.63), channel_id=1, source_target_pairs={{0,7},{1,0},{2,1},{3,2},{4,3},{5,4},{6,5},{7,6}} | collective-permute-start | bytes 1572872 | tf_op jit(solution)/shard_map/ppermute | solution.py:51
  219.4 1.3 copy-start.5
  228.1 17.8 %copy-start.3 = (bf16[2048,512]{1,0:T(8,128)(2,1)S(1)}, bf16[2048,512]{1,0:T(8,128)(2,1)}, u32[]{:S(2)}) copy-start(bf16[2048,512]{1,0:T(8,128)(2,1)} %get-tuple-element.181) | copy-start | bytes 6291460
where the time goes:
time: 263 us; the launch traced here: 262 us
  matrix products  88.5 us (34%)
  waiting for transfers between devices  78.9 us (30%)
  local copies, waits for them, and re-layouts  61.9 us (24%)
  other arithmetic  17.7 us (7%)
  starting transfers between devices  13.1 us (5%)
    ppermute x2, waiting for transfers between devices, loop_body(): v_vis = lax.ppermute(v_vis, 'group', shift_left)  56.2 us
    dot_general x4, matrix products, kernel_block(): jnp.einsum('nd,md->nm', x_rows, x_cols, preferred_element_type=jnp.float32)  40.8 us
    add x2, local copies, waits for them, and re-layouts, kernel_block(): norm_rows[:, None] + norm_cols[None, :] - 2.0 * gram_mat  35.6 us
    ppermute x1, waiting for transfers between devices, local_fn(): x_vis = lax.ppermute(x_vis, 'group', shift_left)  22.8 us
    sub x1, local copies, waits for them, and re-layouts, kernel_block(): norm_rows[:, None] + norm_cols[None, :] - 2.0 * gram_mat  17.7 us
    dot_general x1, matrix products, local_fn(): return y_acc + jnp.dot(kern_far, v_vis, preferred_element_type=jnp.float32)  15.7 us
    add x2, other arithmetic, kernel_block(): norm_rows[:, None] + norm_cols[None, :] - 2.0 * gram_mat  13.7 us
    dot_general x3, matrix products, pair_step(): jnp.einsum('nm,nr->mr', kern_pair, v_loc, preferred_element_type=jnp.floa...  12.9 us
  transfers between devices with their start and end apart: 11, of which 3 were waited for; matrix products, arithmetic and copies ran while one was open for 52% of the time, Pallas kernels for 0%

commit v1 on v0

v1 whole, which is shorter than its diff:
```python
import functools

import jax
import jax.numpy as jnp
from jax import lax
from jax.experimental import pallas as pl
from jax.experimental.pallas import tpu as pltpu
from jax.sharding import PartitionSpec as P

ROWS = 2048
HALF = ROWS // 2
CHUNK = 512
N_CHUNK = ROWS // CHUNK
SUB = 256
FEAT = 512
RHS = 128
LOG2E = 1.4426950408889634
OWN, PAIR = 0, 1
X_ROWS, Y_ROWS = ROWS, ROWS + HALF


def local_kernel(x_hbm, v_hbm, ell_ref, scale_ref, out_ref,
                 x_all, v_all, lhs, norm_lhs, acc, back, consts,
                 load_sem, pair_send, pair_recv, link_send, link_recv,
                 fwd_send, fwd_recv, back_send, back_recv):
    me = lax.axis_index('group')
    core = lax.rem(me, 2)
    chip_x = lax.rem(me // 2, 2)
    chip_y = me // 4
    pair = me + 1 - 2 * core
    neighbour = (me + 2 - 4 * chip_x, me + 4 - 8 * chip_y)

    load_x = pltpu.make_async_copy(x_hbm, x_all.at[pl.ds(0, ROWS)], load_sem.at[0])
    load_v = pltpu.make_async_copy(v_hbm, v_all.at[pl.ds(0, ROWS)], load_sem.at[1])
    load_x.start()
    load_v.start()

    barrier = pltpu.get_barrier_semaphore()
    for peer in (pair,) + neighbour:
        pl.semaphore_signal(barrier, inc=1, device_id={'group': peer}, device_id_type=pl.DeviceIdType.MESH)
    pl.semaphore_wait(barrier, 3)

    def remote(src, dst, send, recv, peer):
        return pltpu.make_async_remote_copy(src_ref=src, dst_ref=dst, send_sem=send, recv_sem=recv,
                                            device_id={'group': peer}, device_id_type=pl.DeviceIdType.MESH)

    def rows_of(block, chunk):
        return pl.ds(pl.multiple_of(block * ROWS + chunk * CHUNK, CHUNK), CHUNK)

    def pair_copies():
        return (remote(x_all.at[pl.ds(0, ROWS)], x_all.at[pl.ds(PAIR * ROWS, ROWS)], pair_send.at[0], pair_recv.at[0], pair),
                remote(v_all.at[pl.ds(0, ROWS)], v_all.at[pl.ds(PAIR * ROWS, ROWS)], pair_send.at[1], pair_recv.at[1], pair))

    def link_copies(axis, chunk):
        src, dst = rows_of(OWN, chunk), rows_of(2 + 2 * axis, chunk)
        return (remote(x_all.at[src], x_all.at[dst], link_send.at[0, axis, chunk], link_recv.at[0, axis, chunk], neighbour[axis]),
                remote(v_all.at[src], v_all.at[dst], link_send.at[1, axis, chunk], link_recv.at[1, axis, chunk], neighbour[axis]))

    def fwd_copies(axis, chunk):
        src, dst = rows_of(2 + 2 * axis, chunk), rows_of(3 + 2 * axis, chunk)
        return (remote(x_all.at[src], x_all.at[dst], fwd_send.at[0, axis, chunk], fwd_recv.at[0, axis, chunk], pair),
                remote(v_all.at[src], v_all.at[dst], fwd_send.at[1, axis, chunk], fwd_recv.at[1, axis, chunk], pair))

    def back_copy(axis):
        return remote(acc.at[pl.ds(ROWS + axis * HALF, HALF)], back.at[pl.ds(axis * HALF, HALF)],
                      back_send.at[axis], back_recv.at[axis], neighbour[axis])

    def chunk_of(axis, step):
        return lax.rem(step + 2 * axis, N_CHUNK)

    load_x.wait()
    load_v.wait()
    for step in range(N_CHUNK):
        for axis in (0, 1):
            for copy in link_copies(axis, (step + 2 * axis) % N_CHUNK):
                copy.start()
        if step == 0:
            for copy in pair_copies():
                copy.start()

    ell = jnp.full((8, 128), ell_ref[0], jnp.float32)
    consts[0] = -LOG2E / (2.0 * (ell * ell))
    consts[1] = jnp.full((8, 128), scale_ref[0], jnp.float32)

    def set_rows(source, target, count):
        @pl.loop(0, count // CHUNK)
        def _(part):
            rows = x_all[pl.ds(pl.multiple_of(source + part * CHUNK, CHUNK), CHUNK), :]
            at = pl.ds(pl.multiple_of(target + part * CHUNK, CHUNK), CHUNK)
            lhs[at, :] = rows * jnp.bfloat16(-2)
            wide = rows.astype(jnp.float32)
            norm_lhs[at, :] = jnp.broadcast_to(jnp.sum(wide * wide, axis=1, keepdims=True), (CHUNK, 128))
            acc[at, :] = jnp.zeros((CHUNK, RHS), jnp.float32)

    def add_columns(row_start, row_count, cols):
        x_col = x_all[cols, :]
        v_col = v_all[cols, :]
        wide = x_col.astype(jnp.float32)
        norm_col = jnp.broadcast_to(jnp.sum(wide * wide, axis=1, keepdims=True), (CHUNK, 128)).T[0:1, :]
        rate = jnp.concatenate([consts[0, 0:1, :]] * (CHUNK // 128), axis=1)
        scale = jnp.concatenate([consts[1, 0:1, :]] * (CHUNK // 128), axis=1)
        parts = [pl.ds(pl.multiple_of(row_start + i * SUB, SUB), SUB) for i in range(row_count // SUB)]
        grams = [lax.dot_general(lhs[rows, :], x_col, (((1,), (1,)), ((), ())), preferred_element_type=jnp.float32)
                 for rows in parts]
        for rows, gram in zip(parts, grams):
            norm_row = jnp.concatenate([norm_lhs[rows, :]] * (CHUNK // 128), axis=1)
            dist = jnp.maximum((norm_row + norm_col) + gram, 0.0)
            kern = (scale * jnp.exp2(dist * rate)).astype(jnp.bfloat16)
            acc[rows, :] += jnp.dot(kern, v_col, preferred_element_type=jnp.float32)

    def block_of(q):
        return 2 + 2 * lax.rem(q, 2) + q // 2

    def cols_of(step, q):
        return rows_of(block_of(q), lax.rem(step + 2 * lax.rem(q, 2), N_CHUNK))

    def receive(step):
        for axis in (0, 1):
            chunk = chunk_of(axis, step)
            for copy in link_copies(axis, chunk):
                copy.wait_recv()
            for copy in fwd_copies(axis, chunk):
                copy.start()

    def receive_forwarded(step):
        for axis in (0, 1):
            for copy in fwd_copies(axis, chunk_of(axis, step)):
                copy.wait_recv()

    def far_columns(step, q):
        add_columns(jnp.where(lax.rem(q, 2) == 0, Y_ROWS, X_ROWS), HALF, cols_of(step, q))

    set_rows(0, 0, ROWS)

    @pl.loop(0, 2 * N_CHUNK)
    def _(c):
        @pl.when(c == N_CHUNK)
        def _():
            for copy in pair_copies():
                copy.wait_recv()
        add_columns(0, ROWS, rows_of(0, c))

    @pl.loop(0, N_CHUNK // 2)
    def _(step):
        receive(step)

        @pl.loop(0, 4)
        def _(q):
            @pl.when(q == 2)
            def _():
                receive_forwarded(step)
            add_columns(0, ROWS, cols_of(step, q))

    set_rows(2 * ROWS, X_ROWS, HALF)
    set_rows(4 * ROWS + HALF, Y_ROWS, HALF)

    @pl.loop(0, N_CHUNK // 2)
    def _(step):
        @pl.loop(0, 4)
        def _(q):
            far_columns(step, q)

    @pl.loop(N_CHUNK // 2, N_CHUNK)
    def _(step):
        receive(step)

        @pl.loop(0, 4)
        def _(q):
            @pl.when(q == 2)
            def _():
                receive_forwarded(step)
            far_columns(step, q)

        @pl.when(step == N_CHUNK - 1)
        def _():
            for axis in (0, 1):
                back_copy(axis).start()

        @pl.loop(0, 4)
        def _(q):
            add_columns(0, ROWS, cols_of(step, q))

    for axis in (0, 1):
        back_copy(axis).wait_recv()
    out_ref[...] = acc[pl.ds(0, ROWS), :] + back[...]

    for copy in pair_copies():
        copy.wait_send()
    for axis in (0, 1):
        back_copy(axis).wait_send()
        for chunk in range(N_CHUNK):
            for copy in link_copies(axis, chunk) + fwd_copies(axis, chunk):
                copy.wait_send()


def solution(mesh):
    row_spec = P(('tasks', 'group'), None)
    dma = pltpu.SemaphoreType.DMA

    def local_fn(x_loc, v_loc, lengthscale, outscale):
        return pl.pallas_call(
            local_kernel,
            out_shape=jax.ShapeDtypeStruct((ROWS, RHS), jnp.float32),
            in_specs=[pl.BlockSpec(memory_space=pl.ANY), pl.BlockSpec(memory_space=pl.ANY),
                      pl.BlockSpec(memory_space=pltpu.SMEM), pl.BlockSpec(memory_space=pltpu.SMEM)],
            out_specs=pl.BlockSpec(memory_space=pltpu.VMEM),
            scratch_shapes=[
                pltpu.VMEM((6 * ROWS, FEAT), jnp.bfloat16),
                pltpu.VMEM((6 * ROWS, RHS), jnp.bfloat16),
                pltpu.VMEM((2 * ROWS, FEAT), jnp.bfloat16),
                pltpu.VMEM((2 * ROWS, 128), jnp.float32),
                pltpu.VMEM((2 * ROWS, RHS), jnp.float32),
                pltpu.VMEM((ROWS, RHS), jnp.float32),
                pltpu.VMEM((2, 8, 128), jnp.float32),
                dma((2,)), dma((2,)), dma((2,)),
                dma((2, 2, N_CHUNK)), dma((2, 2, N_CHUNK)),
                dma((2, 2, N_CHUNK)), dma((2, 2, N_CHUNK)),
                dma((2,)), dma((2,)),
            ],
            compiler_params=pltpu.CompilerParams(collective_id=0, has_side_effects=True, vmem_limit_bytes=60 * 2 ** 20),
        )(x_loc, v_loc, lengthscale, outscale)

    return jax.shard_map(local_fn, mesh=mesh, in_specs=(row_spec, row_spec, P(None), P(None)), out_specs=row_spec, check_vma=False)
```

time: 263 us -> 89.2 us (0.34)
  matrix products: 88.5 us -> 0 us
  Pallas kernels: 0 us -> 85.4 us
  waiting for transfers between devices: 78.9 us -> 0 us
  local copies, waits for them, and re-layouts: 61.9 us -> 2.26 us
  other arithmetic: 17.7 us -> 0 us
  starting transfers between devices: 13.1 us -> 0 us
    dot_general x12 -> x0, matrix products: 88.5 us -> none  [the longest x4 40.8 us: kernel_block(): jnp.einsum('nd,md->nm', x_rows, x_cols, preferred_element_type=jnp.float32)]
    pallas_call x0 -> x1, Pallas kernels: none -> 85.4 us  [local_fn(): pl.pallas_call(local_kernel, out_shape=jax.ShapeDtypeStruct((ROWS, RHS),...]
    ppermute x11 -> x0, waiting for transfers between devices: 78.9 us -> none  [the longest x2 56.2 us: loop_body(): v_vis = lax.ppermute(v_vis, 'group', shift_left)]
    add x2 -> x0, local copies, waits for them, and re-layouts: 35.6 us -> none  [kernel_block(): norm_rows[:, None] + norm_cols[None, :] - 2.0 * gram_mat]
    sub x1 -> x0, local copies, waits for them, and re-layouts: 17.7 us -> none  [kernel_block(): norm_rows[:, None] + norm_cols[None, :] - 2.0 * gram_mat]
    add x2 -> x0, other arithmetic: 13.7 us -> none  [kernel_block(): norm_rows[:, None] + norm_cols[None, :] - 2.0 * gram_mat]
    ppermute x11 -> x0, starting transfers between devices: 13.1 us -> none  [the longest x1 3.74 us: local_fn(): x_vis = lax.ppermute(x_loc, 'group', shift_left)]
    while x8 -> x0, local copies, waits for them, and re-layouts: 6.43 us -> none
  transfers between devices with their start and end apart: 11 -> 0, of which waited for: 3 -> 0; matrix products, arithmetic and copies ran while one was open for 52% -> 0% of each run, Pallas kernels for 0% -> 0%
where the time goes in v1:
time: 89.2 us; the launch traced here: 89 us
  Pallas kernels  85.4 us (96%)
  local copies, waits for them, and re-layouts  2.26 us (3%)
  between operations  1.3 us (1%)
    pallas_call x1, Pallas kernels, local_fn(): pl.pallas_call(local_kernel, out_shape=jax.ShapeDtypeStruct((ROWS, RHS),...  85.4 us
    unnamed x1, local copies, waits for them, and re-layouts  2.26 us

profile of v1, /device:TPU:0, one launch (start us, length us, event | category | flops | bytes accessed | tf_op | source)
XLA Modules:
  0.0 89.0 jit_solution(15727654525747535076)
XLA Ops:
  1.3 85.4 %shard_map.46 = f32[2048,128]{1,0:T(8,128)} custom-call(bf16[2048,512]{1,0:T(8,128)(2,1)} %x_hbm.1, bf16[2048,128]{1,0:T(8,128)(2,1)} %v_hbm.1, f32[1]{0:T(128)S(6)} %copy.6.ell_ref, f32[1]{0:T(128)S(6)} %copy.7.scale_ref), custom_call_target="tpu_custom_call" | custom-call | tf_op jit(solution)/shard_map/pallas_call | solution.py:201
  86.8 2.3 %copy.8 = f32[2048,128]{1,0:T(8,128)} copy(f32[2048,128]{1,0:T(8,128)} %shard_map.46) | data formatting | bytes 2097152

commit v2 on v1

v2 whole, which is shorter than its diff:
```python
import functools

import jax
import jax.numpy as jnp
from jax import lax
from jax.experimental import pallas as pl
from jax.experimental.pallas import tpu as pltpu
from jax.sharding import PartitionSpec as P

ROWS = 2048
HALF = ROWS // 2
CHUNK = 512
PIECE = 256
N_CHUNK = ROWS // CHUNK
N_PIECE = ROWS // PIECE
SUB = 256
FEAT = 512
RHS = 128
LOG2E = 1.4426950408889634
OWN, PAIR = 0, 1
X_ROWS, Y_ROWS = ROWS, ROWS + HALF


def local_kernel(x_hbm, v_hbm, ell_ref, scale_ref, out_ref,
                 x_all, v_all, lhs, norm_lhs, acc, back,
                 load_sem, pair_send, pair_recv, link_send, link_recv,
                 fwd_send, fwd_recv, back_send, back_recv):
    me = lax.axis_index('group')
    core = lax.rem(me, 2)
    chip_x = lax.rem(me // 2, 2)
    chip_y = me // 4
    pair = me + 1 - 2 * core
    neighbour = (me + 2 - 4 * chip_x, me + 4 - 8 * chip_y)

    load_x = pltpu.make_async_copy(x_hbm, x_all.at[pl.ds(0, ROWS)], load_sem.at[0])
    load_v = pltpu.make_async_copy(v_hbm, v_all.at[pl.ds(0, ROWS)], load_sem.at[1])
    load_x.start()
    load_v.start()

    barrier = pltpu.get_barrier_semaphore()
    for peer in (pair,) + neighbour:
        pl.semaphore_signal(barrier, inc=1, device_id={'group': peer}, device_id_type=pl.DeviceIdType.MESH)
    pl.semaphore_wait(barrier, 3)

    def remote(src, dst, send, recv, peer):
        return pltpu.make_async_remote_copy(src_ref=src, dst_ref=dst, send_sem=send, recv_sem=recv,
                                            device_id={'group': peer}, device_id_type=pl.DeviceIdType.MESH)

    def rows_of(block, chunk):
        return pl.ds(pl.multiple_of(block * ROWS + chunk * CHUNK, CHUNK), CHUNK)

    def piece_of(block, piece):
        return pl.ds(pl.multiple_of(block * ROWS + piece * PIECE, PIECE), PIECE)

    def pair_copies():
        return (remote(x_all.at[pl.ds(0, ROWS)], x_all.at[pl.ds(PAIR * ROWS, ROWS)], pair_send.at[0], pair_recv.at[0], pair),
                remote(v_all.at[pl.ds(0, ROWS)], v_all.at[pl.ds(PAIR * ROWS, ROWS)], pair_send.at[1], pair_recv.at[1], pair))

    def link_copies(axis, piece):
        src, dst = piece_of(OWN, piece), piece_of(2 + 2 * axis, piece)
        return (remote(x_all.at[src], x_all.at[dst], link_send.at[0, axis, piece], link_recv.at[0, axis, piece], neighbour[axis]),
                remote(v_all.at[src], v_all.at[dst], link_send.at[1, axis, piece], link_recv.at[1, axis, piece], neighbour[axis]))

    def fwd_copies(axis, piece):
        src, dst = piece_of(2 + 2 * axis, piece), piece_of(3 + 2 * axis, piece)
        return (remote(x_all.at[src], x_all.at[dst], fwd_send.at[0, axis, piece], fwd_recv.at[0, axis, piece], pair),
                remote(v_all.at[src], v_all.at[dst], fwd_send.at[1, axis, piece], fwd_recv.at[1, axis, piece], pair))

    def back_copy(axis):
        return remote(acc.at[pl.ds(ROWS + axis * HALF, HALF)], back.at[pl.ds(axis * HALF, HALF)],
                      back_send.at[axis], back_recv.at[axis], neighbour[axis])

    def chunk_of(axis, step):
        return lax.rem(step + 2 * axis, N_CHUNK)

    def piece_at(axis, step):
        return lax.rem(step + (N_PIECE // 2) * axis, N_PIECE)

    load_x.wait()
    load_v.wait()
    for step in range(N_PIECE):
        for axis in (0, 1):
            for copy in link_copies(axis, (step + N_PIECE // 2 * axis) % N_PIECE):
                copy.start()
        if step == 0:
            for copy in pair_copies():
                copy.start()

    ell = jnp.full((8, 128), ell_ref[0], jnp.float32)
    rate = (-LOG2E / (2.0 * (ell * ell)))[0, 0]
    scale = scale_ref[0]

    def set_rows(source, target, count):
        @pl.loop(0, count // CHUNK)
        def _(part):
            rows = x_all[pl.ds(pl.multiple_of(source + part * CHUNK, CHUNK), CHUNK), :]
            at = pl.ds(pl.multiple_of(target + part * CHUNK, CHUNK), CHUNK)
            lhs[at, :] = rows * jnp.bfloat16(-2)
            wide = rows.astype(jnp.float32)
            norm_lhs[at, :] = jnp.broadcast_to(jnp.sum(wide * wide, axis=1, keepdims=True), (CHUNK, 128))
            acc[at, :] = jnp.zeros((CHUNK, RHS), jnp.float32)

    def add_columns(items, row_count, width, same_rows):
        work = []
        for row_start, cols in items:
            x_col = x_all[cols, :]
            wide = x_col.astype(jnp.float32)
            norm_col = jnp.broadcast_to(jnp.sum(wide * wide, axis=1, keepdims=True), (width, 128)).T[0:1, :]
            for i in range(row_count // SUB):
                rows = pl.ds(pl.multiple_of(row_start + i * SUB, SUB), SUB)
                gram = lax.dot_general(lhs[rows, :], x_col, (((1,), (1,)), ((), ())), preferred_element_type=jnp.float32)
                work.append((rows, cols, norm_col, gram))
        def part_sum(rows, cols, norm_col, gram):
            norm_row = jnp.concatenate([norm_lhs[rows, :]] * (width // 128), axis=1)
            dist = jnp.maximum((norm_row + norm_col) + gram, 0.0)
            kern = (scale * jnp.exp2(dist * rate)).astype(jnp.bfloat16)
            return jnp.dot(kern, v_all[cols, :], preferred_element_type=jnp.float32)
        per_item = row_count // SUB
        if same_rows:
            for i in range(per_item):
                acc[work[i][0], :] += part_sum(*work[i]) + part_sum(*work[per_item + i])
        else:
            for one in work:
                acc[one[0], :] += part_sum(*one)

    def cols_of(axis, forwarded, step):
        return rows_of(2 + 2 * axis + forwarded, chunk_of(axis, step))

    def receive(step):
        for axis in (0, 1):
            piece = piece_at(axis, step)
            for copy in link_copies(axis, piece):
                copy.wait_recv()
            for copy in fwd_copies(axis, piece):
                copy.start()

    def receive_forwarded(step):
        for axis in (0, 1):
            for copy in fwd_copies(axis, piece_at(axis, step)):
                copy.wait_recv()

    def own_columns(step, forwarded):
        add_columns([(0, cols_of(axis, forwarded, step)) for axis in (0, 1)], ROWS, CHUNK, True)

    def own_piece(step, forwarded):
        add_columns([(0, piece_of(2 + 2 * axis + forwarded, piece_at(axis, step))) for axis in (0, 1)], ROWS, PIECE, True)

    def far_columns(step, forwarded):
        add_columns([(Y_ROWS, cols_of(0, forwarded, step)), (X_ROWS, cols_of(1, forwarded, step))], HALF, CHUNK, False)

    def far_piece(step, forwarded):
        add_columns([(Y_ROWS, piece_of(2 + forwarded, piece_at(0, step))),
                     (X_ROWS, piece_of(4 + forwarded, piece_at(1, step)))], HALF, PIECE, False)

    set_rows(0, 0, ROWS)

    @pl.loop(0, N_CHUNK)
    def _(c):
        @pl.when(c == N_CHUNK // 2)
        def _():
            for copy in pair_copies():
                copy.wait_recv()
        add_columns([(0, rows_of(0, 2 * c)), (0, rows_of(0, 2 * c + 1))], ROWS, CHUNK, True)

    @pl.loop(0, N_PIECE // 2)
    def _(step):
        receive(step)

        @pl.loop(0, 2)
        def _(forwarded):
            @pl.when(forwarded == 1)
            def _():
                receive_forwarded(step)
            own_piece(step, forwarded)

    set_rows(2 * ROWS, X_ROWS, HALF)
    set_rows(4 * ROWS + HALF, Y_ROWS, HALF)

    @pl.loop(0, N_CHUNK + 2)
    def _(c):
        step = c // 2

        @pl.when(c == N_CHUNK)
        def _():
            receive(N_PIECE // 2)
            receive(N_PIECE // 2 + 1)

        @pl.when(c == N_CHUNK + 1)
        def _():
            receive_forwarded(N_PIECE // 2)
            receive_forwarded(N_PIECE // 2 + 1)

        far_columns(step, lax.rem(c, 2))

    @pl.loop(N_CHUNK // 2, N_CHUNK)
    def _(half):
        @pl.when(half == N_CHUNK - 1)
        def _():
            @pl.loop(N_PIECE - 2, N_PIECE)
            def _(step):
                receive(step)

                @pl.loop(0, 2)
                def _(forwarded):
                    @pl.when(forwarded == 1)
                    def _():
                        receive_forwarded(step)
                    far_piece(step, forwarded)

            for axis in (0, 1):
                back_copy(axis).start()

        @pl.loop(0, 2)
        def _(forwarded):
            own_columns(half, forwarded)

    for axis in (0, 1):
        back_copy(axis).wait_recv()
    out_ref[...] = acc[pl.ds(0, ROWS), :] + back[...]

    for copy in pair_copies():
        copy.wait_send()
    for axis in (0, 1):
        back_copy(axis).wait_send()
        for piece in range(N_PIECE):
            for copy in link_copies(axis, piece) + fwd_copies(axis, piece):
                copy.wait_send()


def solution(mesh):
    row_spec = P(('tasks', 'group'), None)
    dma = pltpu.SemaphoreType.DMA

    def local_fn(x_loc, v_loc, lengthscale, outscale):
        return pl.pallas_call(
            local_kernel,
            out_shape=pltpu.VMEM((ROWS, RHS), jnp.float32),
            in_specs=[pl.BlockSpec(memory_space=pl.ANY), pl.BlockSpec(memory_space=pl.ANY),
                      pl.BlockSpec(memory_space=pltpu.SMEM), pl.BlockSpec(memory_space=pltpu.SMEM)],
            out_specs=pl.BlockSpec(memory_space=pltpu.VMEM),
            scratch_shapes=[
                pltpu.VMEM((6 * ROWS, FEAT), jnp.bfloat16),
                pltpu.VMEM((6 * ROWS, RHS), jnp.bfloat16),
                pltpu.VMEM((2 * ROWS, FEAT), jnp.bfloat16),
                pltpu.VMEM((2 * ROWS, 128), jnp.float32),
                pltpu.VMEM((2 * ROWS, RHS), jnp.float32),
                pltpu.VMEM((ROWS, RHS), jnp.float32),
                dma((2,)), dma((2,)), dma((2,)),
                dma((2, 2, N_PIECE)), dma((2, 2, N_PIECE)),
                dma((2, 2, N_PIECE)), dma((2, 2, N_PIECE)),
                dma((2,)), dma((2,)),
            ],
            compiler_params=pltpu.CompilerParams(collective_id=0, has_side_effects=True, vmem_limit_bytes=60 * 2 ** 20),
        )(x_loc, v_loc, lengthscale, outscale)

    return jax.shard_map(local_fn, mesh=mesh, in_specs=(row_spec, row_spec, P(None), P(None)), out_specs=row_spec, check_vma=False)
```

time: 89.2 us -> 83.5 us (0.936)
  Pallas kernels: 85.4 us -> 81.2 us
  local copies, waits for them, and re-layouts: 2.26 us -> 0.97 us
    pallas_call x1, Pallas kernels: 85.4 us -> 81.2 us  [local_fn(): pl.pallas_call(local_kernel, out_shape=pltpu.VMEM((ROWS, RHS), jnp.float3...]
    unnamed x1, local copies, waits for them, and re-layouts: 2.26 us -> 0.97 us
where the time goes in v2:
time: 83.5 us; the launch traced here: 83.4 us
  Pallas kernels  81.2 us (97%)
  between operations  1.31 us (2%)
  local copies, waits for them, and re-layouts  0.97 us (1%)
    pallas_call x1, Pallas kernels, local_fn(): pl.pallas_call(local_kernel, out_shape=pltpu.VMEM((ROWS, RHS), jnp.float3...  81.2 us

profile of v2, /device:TPU:0, one launch (start us, length us, event | category | flops | bytes accessed | tf_op | source)
XLA Modules:
  0.0 83.4 jit_solution(10612482903327248273)
XLA Ops:
  1.3 81.2 %shard_map.46 = f32[2048,128]{1,0:T(8,128)S(1)} custom-call(bf16[2048,512]{1,0:T(8,128)(2,1)} %x_hbm.1, bf16[2048,128]{1,0:T(8,128)(2,1)} %v_hbm.1, f32[1]{0:T(128)S(6)} %copy.7.ell_ref, f32[1]{0:T(128)S(6)} %copy.8.scale_ref), custom_call_target="tpu_custom_call" | custom-call | tf_op jit(solution)/shard_map/pallas_call | solution.py:235
  82.5 1.0 %copy.6 = f32[2048,128]{1,0:T(8,128)} copy(f32[2048,128]{1,0:T(8,128)S(1)} %shard_map.46) | data formatting | bytes 2097152

commit v3 on v2

--- a/solution.py
+++ b/solution.py
@@ -11,8 +11,9 @@
 HALF = ROWS // 2
 CHUNK = 512
 PIECE = 256
+TAIL = ((6, 1536, 256), (7, 1792, 128), (8, 1920, 128))
 N_CHUNK = ROWS // CHUNK
-N_PIECE = ROWS // PIECE
+TRANSFERS = tuple((i, i * PIECE, PIECE) for i in range(6)) + TAIL
 SUB = 256
 FEAT = 512
 RHS = 128
@@ -49,42 +50,35 @@
     def rows_of(block, chunk):
         return pl.ds(pl.multiple_of(block * ROWS + chunk * CHUNK, CHUNK), CHUNK)
 
-    def piece_of(block, piece):
-        return pl.ds(pl.multiple_of(block * ROWS + piece * PIECE, PIECE), PIECE)
+    def part_of(block, axis, start, width):
+        return pl.ds(pl.multiple_of(block * ROWS + lax.rem(start + HALF * axis, ROWS), width), width)
 
     def pair_copies():
         return (remote(x_all.at[pl.ds(0, ROWS)], x_all.at[pl.ds(PAIR * ROWS, ROWS)], pair_send.at[0], pair_recv.at[0], pair),
                 remote(v_all.at[pl.ds(0, ROWS)], v_all.at[pl.ds(PAIR * ROWS, ROWS)], pair_send.at[1], pair_recv.at[1], pair))
 
-    def link_copies(axis, piece):
-        src, dst = piece_of(OWN, piece), piece_of(2 + 2 * axis, piece)
-        return (remote(x_all.at[src], x_all.at[dst], link_send.at[0, axis, piece], link_recv.at[0, axis, piece], neighbour[axis]),
-                remote(v_all.at[src], v_all.at[dst], link_send.at[1, axis, piece], link_recv.at[1, axis, piece], neighbour[axis]))
-
-    def fwd_copies(axis, piece):
-        src, dst = piece_of(2 + 2 * axis, piece), piece_of(3 + 2 * axis, piece)
-        return (remote(x_all.at[src], x_all.at[dst], fwd_send.at[0, axis, piece], fwd_recv.at[0, axis, piece], pair),
-                remote(v_all.at[src], v_all.at[dst], fwd_send.at[1, axis, piece], fwd_recv.at[1, axis, piece], pair))
+    def link_copies(axis, index, start, width):
+        src, dst = part_of(OWN, axis, start, width), part_of(2 + 2 * axis, axis, start, width)
+        return (remote(x_hbm.at[src], x_all.at[dst], link_send.at[0, axis, index], link_recv.at[0, axis, index], neighbour[axis]),
+                remote(v_hbm.at[src], v_all.at[dst], link_send.at[1, axis, index], link_recv.at[1, axis, index], neighbour[axis]))
+
+    def fwd_copies(axis, index, start, width):
+        src, dst = part_of(2 + 2 * axis, axis, start, width), part_of(3 + 2 * axis, axis, start, width)
+        return (remote(x_all.at[src], x_all.at[dst], fwd_send.at[0, axis, index], fwd_recv.at[0, axis, index], pair),
+                remote(v_all.at[src], v_all.at[dst], fwd_send.at[1, axis, index], fwd_recv.at[1, axis, index], pair))
 
     def back_copy(axis):
         return remote(acc.at[pl.ds(ROWS + axis * HALF, HALF)], back.at[pl.ds(axis * HALF, HALF)],
                       back_send.at[axis], back_recv.at[axis], neighbour[axis])
 
-    def chunk_of(axis, step):
-        return lax.rem(step + 2 * axis, N_CHUNK)
-
-    def piece_at(axis, step):
-        return lax.rem(step + (N_PIECE // 2) * axis, N_PIECE)
-
+    for index, start, width in TRANSFERS:
+        for axis in (0, 1):
+            for copy in link_copies(axis, index, start, width):
+                copy.start()
     load_x.wait()
     load_v.wait()
-    for step in range(N_PIECE):
-        for axis in (0, 1):
-            for copy in link_copies(axis, (step + N_PIECE // 2 * axis) % N_PIECE):
-                copy.start()
-        if step == 0:
-            for copy in pair_copies():
-                copy.start()
+    for copy in pair_copies():
+        copy.start()
 
     ell = jnp.full((8, 128), ell_ref[0], jnp.float32)
     rate = (-LOG2E / (2.0 * (ell * ell)))[0, 0]
@@ -123,34 +117,24 @@
             for one in work:
                 acc[one[0], :] += part_sum(*one)
 
-    def cols_of(axis, forwarded, step):
-        return rows_of(2 + 2 * axis + forwarded, chunk_of(axis, step))
-
-    def receive(step):
+    def receive(index, start, width):
         for axis in (0, 1):
-            piece = piece_at(axis, step)
-            for copy in link_copies(axis, piece):
+            for copy in link_copies(axis, index, start, width):
                 copy.wait_recv()
-            for copy in fwd_copies(axis, piece):
+            for copy in fwd_copies(axis, index, start, width):
                 copy.start()
 
-    def receive_forwarded(step):
+    def receive_forwarded(index, start, width):
         for axis in (0, 1):
-            for copy in fwd_copies(axis, piece_at(axis, step)):
+            for copy in fwd_copies(axis, index, start, width):
                 copy.wait_recv()
 
-    def own_columns(step, forwarded):
-        add_columns([(0, cols_of(axis, forwarded, step)) for axis in (0, 1)], ROWS, CHUNK, True)
-
-    def own_piece(step, forwarded):
-        add_columns([(0, piece_of(2 + 2 * axis + forwarded, piece_at(axis, step))) for axis in (0, 1)], ROWS, PIECE, True)
-
-    def far_columns(step, forwarded):
-        add_columns([(Y_ROWS, cols_of(0, forwarded, step)), (X_ROWS, cols_of(1, forwarded, step))], HALF, CHUNK, False)
-
-    def far_piece(step, forwarded):
-        add_columns([(Y_ROWS, piece_of(2 + forwarded, piece_at(0, step))),
-                     (X_ROWS, piece_of(4 + forwarded, piece_at(1, step)))], HALF, PIECE, False)
+    def own_columns(start, width, forwarded):
+        add_columns([(0, part_of(2 + 2 * axis + forwarded, axis, start, width)) for axis in (0, 1)], ROWS, width, True)
+
+    def far_columns(start, width, forwarded):
+        add_columns([(Y_ROWS, part_of(2 + forwarded, 0, start, width)),
+                     (X_ROWS, part_of(4 + forwarded, 1, start, width))], HALF, width, False)
 
     set_rows(0, 0, ROWS)
 
@@ -162,57 +146,52 @@
                 copy.wait_recv()
         add_columns([(0, rows_of(0, 2 * c)), (0, rows_of(0, 2 * c + 1))], ROWS, CHUNK, True)
 
-    @pl.loop(0, N_PIECE // 2)
-    def _(step):
-        receive(step)
+    @pl.loop(0, HALF // PIECE)
+    def _(index):
+        receive(index, index * PIECE, PIECE)
 
         @pl.loop(0, 2)
         def _(forwarded):
             @pl.when(forwarded == 1)
             def _():
-                receive_forwarded(step)
-            own_piece(step, forwarded)
+                receive_forwarded(index, index * PIECE, PIECE)
+            own_columns(index * PIECE, PIECE, forwarded)
 
     set_rows(2 * ROWS, X_ROWS, HALF)
     set_rows(4 * ROWS + HALF, Y_ROWS, HALF)
 
-    @pl.loop(0, N_CHUNK + 2)
+    @pl.loop(0, 6)
     def _(c):
-        step = c // 2
-
-        @pl.when(c == N_CHUNK)
-        def _():
-            receive(N_PIECE // 2)
-            receive(N_PIECE // 2 + 1)
-
-        @pl.when(c == N_CHUNK + 1)
-        def _():
-            receive_forwarded(N_PIECE // 2)
-            receive_forwarded(N_PIECE // 2 + 1)
-
-        far_columns(step, lax.rem(c, 2))
-
-    @pl.loop(N_CHUNK // 2, N_CHUNK)
-    def _(half):
-        @pl.when(half == N_CHUNK - 1)
-        def _():
-            @pl.loop(N_PIECE - 2, N_PIECE)
-            def _(step):
-                receive(step)
+        @pl.when(c == 4)
+        def _():
+            receive(4, HALF, PIECE)
+            receive(5, HALF + PIECE, PIECE)
+
+        @pl.when(c == 5)
+        def _():
+            receive_forwarded(4, HALF, PIECE)
+            receive_forwarded(5, HALF + PIECE, PIECE)
+
+        far_columns(c // 2 * CHUNK, CHUNK, lax.rem(c, 2))
+
+    @pl.loop(0, 4)
+    def _(c):
+        @pl.when(c == 1)
+        def _():
+            for index, start, width in TAIL:
+                receive(index, start, width)
 
                 @pl.loop(0, 2)
                 def _(forwarded):
                     @pl.when(forwarded == 1)
                     def _():
-                        receive_forwarded(step)
-                    far_piece(step, forwarded)
+                        receive_forwarded(index, start, width)
+                    far_columns(start, width, forwarded)
 
             for axis in (0, 1):
                 back_copy(axis).start()
 
-        @pl.loop(0, 2)
-        def _(forwarded):
-            own_columns(half, forwarded)
+        own_columns(HALF + c // 2 * CHUNK, CHUNK, lax.rem(c, 2))
 
     for axis in (0, 1):
         back_copy(axis).wait_recv()
@@ -222,8 +201,8 @@
         copy.wait_send()
     for axis in (0, 1):
         back_copy(axis).wait_send()
-        for piece in range(N_PIECE):
-            for copy in link_copies(axis, piece) + fwd_copies(axis, piece):
+        for transfer in TRANSFERS:
+            for copy in link_copies(axis, *transfer) + fwd_copies(axis, *transfer):
                 copy.wait_send()
 
 
@@ -246,8 +225,8 @@
                 pltpu.VMEM((2 * ROWS, RHS), jnp.float32),
                 pltpu.VMEM((ROWS, RHS), jnp.float32),
                 dma((2,)), dma((2,)), dma((2,)),
-                dma((2, 2, N_PIECE)), dma((2, 2, N_PIECE)),
-                dma((2, 2, N_PIECE)), dma((2, 2, N_PIECE)),
+                dma((2, 2, len(TRANSFERS))), dma((2, 2, len(TRANSFERS))),
+                dma((2, 2, len(TRANSFERS))), dma((2, 2, len(TRANSFERS))),
                 dma((2,)), dma((2,)),
             ],
             compiler_params=pltpu.CompilerParams(collective_id=0, has_side_effects=True, vmem_limit_bytes=60 * 2 ** 20),

time: 83.5 us -> 80.8 us (0.968)
  Pallas kernels: 81.2 us -> 78.4 us
    pallas_call x1, Pallas kernels: 81.2 us -> 78.4 us  [local_fn(): pl.pallas_call(local_kernel, out_shape=pltpu.VMEM((ROWS, RHS), jnp.float3...]
where the time goes in v3:
time: 80.8 us; the launch traced here: 80.7 us
  Pallas kernels  78.4 us (97%)
  between operations  1.31 us (2%)
  local copies, waits for them, and re-layouts  0.97 us (1%)
    pallas_call x1, Pallas kernels, local_fn(): pl.pallas_call(local_kernel, out_shape=pltpu.VMEM((ROWS, RHS), jnp.float3...  78.4 us

profile of v3, /device:TPU:0, one launch (start us, length us, event | category | flops | bytes accessed | tf_op | source)
XLA Modules:
  0.0 80.7 jit_solution(16046907688405354015)
XLA Ops:
  1.3 78.4 %shard_map.46 = f32[2048,128]{1,0:T(8,128)S(1)} custom-call(bf16[2048,512]{1,0:T(8,128)(2,1)} %x_hbm.1, bf16[2048,128]{1,0:T(8,128)(2,1)} %v_hbm.1, f32[1]{0:T(128)S(6)} %copy.7.ell_ref, f32[1]{0:T(128)S(6)} %copy.8.scale_ref), custom_call_target="tpu_custom_call" | custom-call | tf_op jit(solution)/shard_map/pallas_call | solution.py:214
  79.7 1.0 %copy.6 = f32[2048,128]{1,0:T(8,128)} copy(f32[2048,128]{1,0:T(8,128)S(1)} %shard_map.46) | data formatting | bytes 2097152

commit v4 on v3

--- a/solution.py
+++ b/solution.py
@@ -15,6 +15,7 @@
 N_CHUNK = ROWS // CHUNK
 TRANSFERS = tuple((i, i * PIECE, PIECE) for i in range(6)) + TAIL
 SUB = 256
+GROUPS = ((0, 256), (256, 768))
 FEAT = 512
 RHS = 128
 LOG2E = 1.4426950408889634
@@ -23,7 +24,7 @@
 
 
 def local_kernel(x_hbm, v_hbm, ell_ref, scale_ref, out_ref,
-                 x_all, v_all, lhs, norm_lhs, acc, back,
+                 x_all, v_all, lhs, norm_lhs, norm_cols, acc, back,
                  load_sem, pair_send, pair_recv, link_send, link_recv,
                  fwd_send, fwd_recv, back_send, back_recv):
     me = lax.axis_index('group')
@@ -67,9 +68,10 @@
         return (remote(x_all.at[src], x_all.at[dst], fwd_send.at[0, axis, index], fwd_recv.at[0, axis, index], pair),
                 remote(v_all.at[src], v_all.at[dst], fwd_send.at[1, axis, index], fwd_recv.at[1, axis, index], pair))
 
-    def back_copy(axis):
-        return remote(acc.at[pl.ds(ROWS + axis * HALF, HALF)], back.at[pl.ds(axis * HALF, HALF)],
-                      back_send.at[axis], back_recv.at[axis], neighbour[axis])
+    def back_copy(axis, group):
+        first, count = GROUPS[group]
+        return remote(acc.at[pl.ds(ROWS + axis * HALF + first, count)], back.at[pl.ds(axis * HALF + first, count)],
+                      back_send.at[axis, group], back_recv.at[axis, group], neighbour[axis])
 
     for index, start, width in TRANSFERS:
         for axis in (0, 1):
@@ -94,12 +96,17 @@
             norm_lhs[at, :] = jnp.broadcast_to(jnp.sum(wide * wide, axis=1, keepdims=True), (CHUNK, 128))
             acc[at, :] = jnp.zeros((CHUNK, RHS), jnp.float32)
 
-    def add_columns(items, row_count, width, same_rows):
+    def add_columns(items, row_count, width, same_rows, known_norms, keep_norms=True):
         work = []
         for row_start, cols in items:
             x_col = x_all[cols, :]
-            wide = x_col.astype(jnp.float32)
-            norm_col = jnp.broadcast_to(jnp.sum(wide * wide, axis=1, keepdims=True), (width, 128)).T[0:1, :]
+            if known_norms:
+                norm_col = norm_cols[0:1, cols]
+            else:
+                wide = x_col.astype(jnp.float32)
+                norm_col = jnp.broadcast_to(jnp.sum(wide * wide, axis=1, keepdims=True), (width, 128)).T[0:1, :]
+                if keep_norms:
+                    norm_cols[0:1, cols] = norm_col
             for i in range(row_count // SUB):
                 rows = pl.ds(pl.multiple_of(row_start + i * SUB, SUB), SUB)
                 gram = lax.dot_general(lhs[rows, :], x_col, (((1,), (1,)), ((), ())), preferred_element_type=jnp.float32)
@@ -129,12 +136,12 @@
             for copy in fwd_copies(axis, index, start, width):
                 copy.wait_recv()
 
-    def own_columns(start, width, forwarded):
-        add_columns([(0, part_of(2 + 2 * axis + forwarded, axis, start, width)) for axis in (0, 1)], ROWS, width, True)
-
-    def far_columns(start, width, forwarded):
-        add_columns([(Y_ROWS, part_of(2 + forwarded, 0, start, width)),
-                     (X_ROWS, part_of(4 + forwarded, 1, start, width))], HALF, width, False)
+    def own_columns(start, width, forwarded, known_norms):
+        add_columns([(0, part_of(2 + 2 * axis + forwarded, axis, start, width)) for axis in (0, 1)], ROWS, width, True, known_norms)
+
+    def far_columns(start, width, forwarded, known_norms, first=0, count=HALF):
+        add_columns([(Y_ROWS + first, part_of(2 + forwarded, 0, start, width)),
+                     (X_ROWS + first, part_of(4 + forwarded, 1, start, width))], count, width, False, known_norms)
 
     set_rows(0, 0, ROWS)
 
@@ -144,7 +151,7 @@
         def _():
             for copy in pair_copies():
                 copy.wait_recv()
-        add_columns([(0, rows_of(0, 2 * c)), (0, rows_of(0, 2 * c + 1))], ROWS, CHUNK, True)
+        add_columns([(0, rows_of(0, 2 * c)), (0, rows_of(0, 2 * c + 1))], ROWS, CHUNK, True, False, False)
 
     @pl.loop(0, HALF // PIECE)
     def _(index):
@@ -155,30 +162,31 @@
             @pl.when(forwarded == 1)
             def _():
                 receive_forwarded(index, index * PIECE, PIECE)
-            own_columns(index * PIECE, PIECE, forwarded)
+            own_columns(index * PIECE, PIECE, forwarded, False)
 
     set_rows(2 * ROWS, X_ROWS, HALF)
     set_rows(4 * ROWS + HALF, Y_ROWS, HALF)
 
-    @pl.loop(0, 6)
+    @pl.loop(0, 4)
     def _(c):
-        @pl.when(c == 4)
-        def _():
-            receive(4, HALF, PIECE)
-            receive(5, HALF + PIECE, PIECE)
-
-        @pl.when(c == 5)
+        far_columns(c // 2 * CHUNK, CHUNK, lax.rem(c, 2), True)
+
+    receive(4, HALF, PIECE)
+    receive(5, HALF + PIECE, PIECE)
+
+    @pl.loop(0, 2)
+    def _(forwarded):
+        @pl.when(forwarded == 1)
         def _():
             receive_forwarded(4, HALF, PIECE)
             receive_forwarded(5, HALF + PIECE, PIECE)
-
-        far_columns(c // 2 * CHUNK, CHUNK, lax.rem(c, 2))
+        far_columns(HALF, CHUNK, forwarded, False)
 
     @pl.loop(0, 4)
     def _(c):
         @pl.when(c == 1)
         def _():
-            for index, start, width in TAIL:
+            for index, start, width in TAIL[:-1]:
                 receive(index, start, width)
 
                 @pl.loop(0, 2)
@@ -186,21 +194,30 @@
                     @pl.when(forwarded == 1)
                     def _():
                         receive_forwarded(index, start, width)
-                    far_columns(start, width, forwarded)
-
-            for axis in (0, 1):
-                back_copy(axis).start()
-
-        own_columns(HALF + c // 2 * CHUNK, CHUNK, lax.rem(c, 2))
-
-    for axis in (0, 1):
-        back_copy(axis).wait_recv()
-    out_ref[...] = acc[pl.ds(0, ROWS), :] + back[...]
+                    far_columns(start, width, forwarded, False)
+
+            index, start, width = TAIL[-1]
+            receive(index, start, width)
+            far_columns(start, width, 0, False)
+            receive_forwarded(index, start, width)
+            for group, (first, count) in enumerate(GROUPS):
+                far_columns(start, width, 1, group > 0, first, count)
+                for axis in (0, 1):
+                    back_copy(axis, group).start()
+
+        own_columns(HALF + c // 2 * CHUNK, CHUNK, lax.rem(c, 2), True)
+
+    for group, (first, count) in enumerate(GROUPS):
+        for axis in (0, 1):
+            back_copy(axis, group).wait_recv()
+            rows = pl.ds(axis * HALF + first, count)
+            out_ref[rows, :] = acc[rows, :] + back[rows, :]
 
     for copy in pair_copies():
         copy.wait_send()
     for axis in (0, 1):
-        back_copy(axis).wait_send()
+        for group in range(len(GROUPS)):
+            back_copy(axis, group).wait_send()
         for transfer in TRANSFERS:
             for copy in link_copies(axis, *transfer) + fwd_copies(axis, *transfer):
                 copy.wait_send()
@@ -222,12 +239,13 @@
                 pltpu.VMEM((6 * ROWS, RHS), jnp.bfloat16),
                 pltpu.VMEM((2 * ROWS, FEAT), jnp.bfloat16),
                 pltpu.VMEM((2 * ROWS, 128), jnp.float32),
+                pltpu.VMEM((8, 6 * ROWS), jnp.float32),
                 pltpu.VMEM((2 * ROWS, RHS), jnp.float32),
                 pltpu.VMEM((ROWS, RHS), jnp.float32),
                 dma((2,)), dma((2,)), dma((2,)),
                 dma((2, 2, len(TRANSFERS))), dma((2, 2, len(TRANSFERS))),
                 dma((2, 2, len(TRANSFERS))), dma((2, 2, len(TRANSFERS))),
-                dma((2,)), dma((2,)),
+                dma((2, len(GROUPS))), dma((2, len(GROUPS))),
             ],
             compiler_params=pltpu.CompilerParams(collective_id=0, has_side_effects=True, vmem_limit_bytes=60 * 2 ** 20),
         )(x_loc, v_loc, lengthscale, outscale)

time: 80.8 us -> 80.4 us (level)
  no operation moved by 1% of the time
where the time goes in v4:
time: 80.4 us; the launch traced here: 80.3 us
  Pallas kernels  78 us (97%)
  between operations  1.31 us (2%)
  local copies, waits for them, and re-layouts  0.97 us (1%)
    pallas_call x1, Pallas kernels, local_fn(): pl.pallas_call(local_kernel, out_shape=pltpu.VMEM((ROWS, RHS), jnp.float3...  78 us

profile of v4, /device:TPU:0, one launch (start us, length us, event | category | flops | bytes accessed | tf_op | source)
XLA Modules:
  0.0 80.3 jit_solution(15048097428701523281)
XLA Ops:
  1.3 78.0 %shard_map.46 = f32[2048,128]{1,0:T(8,128)S(1)} custom-call(bf16[2048,512]{1,0:T(8,128)(2,1)} %x_hbm.1, bf16[2048,128]{1,0:T(8,128)(2,1)} %v_hbm.1, f32[1]{0:T(128)S(6)} %copy.7.ell_ref, f32[1]{0:T(128)S(6)} %copy.8.scale_ref), custom_call_target="tpu_custom_call" | custom-call | tf_op jit(solution)/shard_map/pallas_call | solution.py:231
  79.3 1.0 %copy.6 = f32[2048,128]{1,0:T(8,128)} copy(f32[2048,128]{1,0:T(8,128)S(1)} %shard_map.46) | data formatting | bytes 2097152

commit v5 on v4

--- a/solution.py
+++ b/solution.py
@@ -11,9 +11,9 @@
 HALF = ROWS // 2
 CHUNK = 512
 PIECE = 256
-TAIL = ((6, 1536, 256), (7, 1792, 128), (8, 1920, 128))
+TAIL = ((3, 1536, 256), (4, 1792, 256))
 N_CHUNK = ROWS // CHUNK
-TRANSFERS = tuple((i, i * PIECE, PIECE) for i in range(6)) + TAIL
+TRANSFERS = ((0, 0, CHUNK), (1, CHUNK, CHUNK), (2, HALF, CHUNK)) + TAIL
 SUB = 256
 GROUPS = ((0, 256), (256, 768))
 FEAT = 512
@@ -153,16 +153,16 @@
                 copy.wait_recv()
         add_columns([(0, rows_of(0, 2 * c)), (0, rows_of(0, 2 * c + 1))], ROWS, CHUNK, True, False, False)
 
-    @pl.loop(0, HALF // PIECE)
+    @pl.loop(0, HALF // CHUNK)
     def _(index):
-        receive(index, index * PIECE, PIECE)
+        receive(index, index * CHUNK, CHUNK)
 
         @pl.loop(0, 2)
         def _(forwarded):
             @pl.when(forwarded == 1)
             def _():
-                receive_forwarded(index, index * PIECE, PIECE)
-            own_columns(index * PIECE, PIECE, forwarded, False)
+                receive_forwarded(index, index * CHUNK, CHUNK)
+            own_columns(index * CHUNK, CHUNK, forwarded, False)
 
     set_rows(2 * ROWS, X_ROWS, HALF)
     set_rows(4 * ROWS + HALF, Y_ROWS, HALF)
@@ -171,15 +171,13 @@
     def _(c):
         far_columns(c // 2 * CHUNK, CHUNK, lax.rem(c, 2), True)
 
-    receive(4, HALF, PIECE)
-    receive(5, HALF + PIECE, PIECE)
+    receive(2, HALF, CHUNK)
 
     @pl.loop(0, 2)
     def _(forwarded):
         @pl.when(forwarded == 1)
         def _():
-            receive_forwarded(4, HALF, PIECE)
-            receive_forwarded(5, HALF + PIECE, PIECE)
+            receive_forwarded(2, HALF, CHUNK)
         far_columns(HALF, CHUNK, forwarded, False)
 
     @pl.loop(0, 4)
@@ -198,9 +196,10 @@
 
             index, start, width = TAIL[-1]
             receive(index, start, width)
-            far_columns(start, width, 0, False)
-            receive_forwarded(index, start, width)
             for group, (first, count) in enumerate(GROUPS):
+                far_columns(start, width, 0, group > 0, first, count)
+                if group == 0:
+                    receive_forwarded(index, start, width)
                 far_columns(start, width, 1, group > 0, first, count)
                 for axis in (0, 1):
                     back_copy(axis, group).start()

time: 80.4 us -> 79.6 us (0.990)
  no operation moved by 1% of the time
where the time goes in v5:
time: 79.6 us; the launch traced here: 79.5 us
  Pallas kernels  77.3 us (97%)
  between operations  1.31 us (2%)
  local copies, waits for them, and re-layouts  0.97 us (1%)
    pallas_call x1, Pallas kernels, local_fn(): pl.pallas_call(local_kernel, out_shape=pltpu.VMEM((ROWS, RHS), jnp.float3...  77.3 us

profile of v5, /device:TPU:0, one launch (start us, length us, event | category | flops | bytes accessed | tf_op | source)
XLA Modules:
  0.0 79.5 jit_solution(15382797625296549888)
XLA Ops:
  1.3 77.3 %shard_map.46 = f32[2048,128]{1,0:T(8,128)S(1)} custom-call(bf16[2048,512]{1,0:T(8,128)(2,1)} %x_hbm.1, bf16[2048,128]{1,0:T(8,128)(2,1)} %v_hbm.1, f32[1]{0:T(128)S(6)} %copy.7.ell_ref, f32[1]{0:T(128)S(6)} %copy.8.scale_ref), custom_call_target="tpu_custom_call" | custom-call | tf_op jit(solution)/shard_map/pallas_call | solution.py:230
  78.6 1.0 %copy.6 = f32[2048,128]{1,0:T(8,128)} copy(f32[2048,128]{1,0:T(8,128)S(1)} %shard_map.46) | data formatting | bytes 2097152

commit v6 on v5

--- a/solution.py
+++ b/solution.py
@@ -58,15 +58,20 @@
         return (remote(x_all.at[pl.ds(0, ROWS)], x_all.at[pl.ds(PAIR * ROWS, ROWS)], pair_send.at[0], pair_recv.at[0], pair),
                 remote(v_all.at[pl.ds(0, ROWS)], v_all.at[pl.ds(PAIR * ROWS, ROWS)], pair_send.at[1], pair_recv.at[1], pair))
 
+    def both(index, axis, src_block, dst_block, start, width, x_src, v_src, send, recv, peer):
+        copies = (remote(x_src.at[part_of(src_block, axis, start, width)], x_all.at[part_of(dst_block, axis, start, width)],
+                         send.at[0, axis, index], recv.at[0, axis, index], peer),)
+        if isinstance(index, int) and index == TAIL[-1][0]:
+            return copies
+        rows = CHUNK
+        return copies + (remote(v_src.at[part_of(src_block, axis, start, rows)], v_all.at[part_of(dst_block, axis, start, rows)],
+                                send.at[1, axis, index], recv.at[1, axis, index], peer),)
+
     def link_copies(axis, index, start, width):
-        src, dst = part_of(OWN, axis, start, width), part_of(2 + 2 * axis, axis, start, width)
-        return (remote(x_hbm.at[src], x_all.at[dst], link_send.at[0, axis, index], link_recv.at[0, axis, index], neighbour[axis]),
-                remote(v_hbm.at[src], v_all.at[dst], link_send.at[1, axis, index], link_recv.at[1, axis, index], neighbour[axis]))
+        return both(index, axis, OWN, 2 + 2 * axis, start, width, x_hbm, v_hbm, link_send, link_recv, neighbour[axis])
 
     def fwd_copies(axis, index, start, width):
-        src, dst = part_of(2 + 2 * axis, axis, start, width), part_of(3 + 2 * axis, axis, start, width)
-        return (remote(x_all.at[src], x_all.at[dst], fwd_send.at[0, axis, index], fwd_recv.at[0, axis, index], pair),
-                remote(v_all.at[src], v_all.at[dst], fwd_send.at[1, axis, index], fwd_recv.at[1, axis, index], pair))
+        return both(index, axis, 2 + 2 * axis, 3 + 2 * axis, start, width, x_all, v_all, fwd_send, fwd_recv, pair)
 
     def back_copy(axis, group):
         first, count = GROUPS[group]

time: 79.6 us -> 79.5 us (level)
  no operation moved by 1% of the time
where the time goes in v6:
time: 79.5 us; the launch traced here: 79.4 us
  Pallas kernels  77.1 us (97%)
  between operations  1.31 us (2%)
  local copies, waits for them, and re-layouts  0.97 us (1%)
    pallas_call x1, Pallas kernels, local_fn(): pl.pallas_call(local_kernel, out_shape=pltpu.VMEM((ROWS, RHS), jnp.float3...  77.1 us

profile of v6, /device:TPU:0, one launch (start us, length us, event | category | flops | bytes accessed | tf_op | source)
XLA Modules:
  0.0 79.4 jit_solution(11367865093783975866)
XLA Ops:
  1.3 77.1 %shard_map.46 = f32[2048,128]{1,0:T(8,128)S(1)} custom-call(bf16[2048,512]{1,0:T(8,128)(2,1)} %x_hbm.1, bf16[2048,128]{1,0:T(8,128)(2,1)} %v_hbm.1, f32[1]{0:T(128)S(6)} %copy.7.ell_ref, f32[1]{0:T(128)S(6)} %copy.8.scale_ref), custom_call_target="tpu_custom_call" | custom-call | tf_op jit(solution)/shard_map/pallas_call | solution.py:235
  78.4 1.0 %copy.6 = f32[2048,128]{1,0:T(8,128)} copy(f32[2048,128]{1,0:T(8,128)S(1)} %shard_map.46) | data formatting | bytes 2097152

commit v7 on v6

--- a/solution.py
+++ b/solution.py
@@ -61,9 +61,9 @@
     def both(index, axis, src_block, dst_block, start, width, x_src, v_src, send, recv, peer):
         copies = (remote(x_src.at[part_of(src_block, axis, start, width)], x_all.at[part_of(dst_block, axis, start, width)],
                          send.at[0, axis, index], recv.at[0, axis, index], peer),)
-        if isinstance(index, int) and index == TAIL[-1][0]:
+        if isinstance(index, int) and index >= TAIL[0][0]:
             return copies
-        rows = CHUNK
+        rows = HALF if isinstance(index, int) and index == TAIL[0][0] - 1 else CHUNK
         return copies + (remote(v_src.at[part_of(src_block, axis, start, rows)], v_all.at[part_of(dst_block, axis, start, rows)],
                                 send.at[1, axis, index], recv.at[1, axis, index], peer),)
 

time: 79.5 us -> 81.1 us (1.020)
  Pallas kernels: 77.1 us -> 78.7 us
    pallas_call x1, Pallas kernels: 77.1 us -> 78.7 us  [local_fn(): pl.pallas_call(local_kernel, out_shape=pltpu.VMEM((ROWS, RHS), jnp.float3...]
where the time goes in v7:
time: 81.1 us; the launch traced here: 81 us
  Pallas kernels  78.7 us (97%)
  between operations  1.31 us (2%)
  local copies, waits for them, and re-layouts  0.97 us (1%)
    pallas_call x1, Pallas kernels, local_fn(): pl.pallas_call(local_kernel, out_shape=pltpu.VMEM((ROWS, RHS), jnp.float3...  78.7 us

profile of v7, /device:TPU:0, one launch (start us, length us, event | category | flops | bytes accessed | tf_op | source)
XLA Modules:
  0.0 81.0 jit_solution(16068283951783405606)
XLA Ops:
  1.3 78.7 %shard_map.46 = f32[2048,128]{1,0:T(8,128)S(1)} custom-call(bf16[2048,512]{1,0:T(8,128)(2,1)} %x_hbm.1, bf16[2048,128]{1,0:T(8,128)(2,1)} %v_hbm.1, f32[1]{0:T(128)S(6)} %copy.7.ell_ref, f32[1]{0:T(128)S(6)} %copy.8.scale_ref), custom_call_target="tpu_custom_call" | custom-call | tf_op jit(solution)/shard_map/pallas_call | solution.py:235
  80.0 1.0 %copy.6 = f32[2048,128]{1,0:T(8,128)} copy(f32[2048,128]{1,0:T(8,128)S(1)} %shard_map.46) | data formatting | bytes 2097152
